TPU v7x, 8 devices: a whole 2x2x1 slice. The times are simulated.
8 devices in a mesh: data: 8 (over z, y, x, core).
Axes of the slice: x: 2, y: 2, z: 1, core: 2. Of those that a mesh axis runs over, the one named last changes fastest.
Arguments:
- x_tokens: bfloat16 [32768, 2048], P('data')
- dh_out: bfloat16 [32768, 2048], P('data')
- w_up: bfloat16 [2, 2048, 5632], replicated
- w_down: bfloat16 [2, 5632, 2048], replicated
- proj_up: bfloat16 [2, 2048, 512], replicated
- proj_down: bfloat16 [2, 2048, 512], replicated
- mom_up: float32 [2, 512, 5632], P(None, None, 'data')
- var_up: float32 [2, 512, 5632], P(None, None, 'data')
- mom_down: float32 [2, 5632, 512], P(None, 'data')
- var_down: float32 [2, 5632, 512], P(None, 'data')
Outputs:
- output 1: bfloat16 [2, 2048, 5632], replicated
- output 2: bfloat16 [2, 5632, 2048], replicated
- output 3: float32 [2, 512, 5632], P(None, None, 'data')
- output 4: float32 [2, 512, 5632], P(None, None, 'data')
- output 5: float32 [2, 5632, 512], P(None, 'data')
- output 6: float32 [2, 5632, 512], P(None, 'data')
All inputs are finite; a program needn't handle non-finite values.
Results may differ from a plain program's by a relative error of at most 0.00729786.
Values are sent between devices in bfloat16 or wider.
A program may use at most 1 GiB of HBM per device.

v0:
```python
import jax
import jax.numpy as jnp
from jax import lax
from jax.sharding import PartitionSpec as P

BETA_ONE = 0.9
BETA_TWO = 0.999
EPSILON = 1e-8
STEP = 4
LEARN_RATE = 0.02
ALPHA_SCALE = 0.25


def contract_rows(lhs, rhs):
    return lax.dot_general(lhs, rhs, (((0,), (0,)), ((), ())), preferred_element_type=jnp.float32)


def contract_cols(lhs, rhs):
    return lax.dot_general(lhs, rhs, (((1,), (1,)), ((), ())), preferred_element_type=jnp.float32)


def projected_grads(x_rows, dh_rows, w_up, w_down, proj_up, proj_down):
    layers = w_up.shape[0]
    hidden = [x_rows]
    act_list = []
    pull_list = []
    for layer_idx in range(layers):
        pre_act = jnp.dot(hidden[layer_idx], w_up[layer_idx], preferred_element_type=jnp.float32)
        gelu_val, gelu_pull = jax.vjp(jax.nn.gelu, pre_act)
        act_val = gelu_val.astype(jnp.bfloat16)
        down_out = jnp.dot(act_val, w_down[layer_idx], preferred_element_type=jnp.float32)
        hidden.append((hidden[layer_idx] + down_out).astype(jnp.bfloat16))
        act_list.append(act_val)
        pull_list.append(gelu_pull)
    grad_rows = dh_rows
    up_parts = [None] * layers
    down_parts = [None] * layers
    for layer_idx in reversed(range(layers)):
        v_proj = jnp.dot(grad_rows, proj_down[layer_idx], preferred_element_type=jnp.float32).astype(jnp.bfloat16)
        down_parts[layer_idx] = contract_rows(act_list[layer_idx], v_proj)
        d_act = contract_cols(grad_rows, w_down[layer_idx])
        d_pre = pull_list[layer_idx](d_act)[0].astype(jnp.bfloat16)
        u_proj = jnp.dot(hidden[layer_idx], proj_up[layer_idx], preferred_element_type=jnp.float32).astype(jnp.bfloat16)
        up_parts[layer_idx] = contract_rows(u_proj, d_pre)
        if layer_idx > 0:
            grad_rows = (grad_rows + contract_cols(d_pre, w_up[layer_idx])).astype(jnp.bfloat16)
    return jnp.stack(up_parts), jnp.stack(down_parts)


def adam_shard(moment, variance, grad_red):
    new_mom = BETA_ONE * moment + (1.0 - BETA_ONE) * grad_red
    new_var = BETA_TWO * variance + (1.0 - BETA_TWO) * grad_red * grad_red
    bias_one = 1.0 - BETA_ONE ** STEP
    bias_two = 1.0 - BETA_TWO ** STEP
    direction = (new_mom / bias_one) / (jnp.sqrt(new_var / bias_two) + EPSILON)
    return new_mom, new_var, direction.astype(jnp.bfloat16)


def solution(mesh):
    def local_step(x_loc, dh_loc, w_up, w_down, proj_up, proj_down, mom_up, var_up, mom_down, var_down):
        micro = x_loc.shape[0] // 2
        scattered = []
        for micro_idx in range(2):
            x_micro = x_loc[micro_idx * micro:(micro_idx + 1) * micro]
            dh_micro = dh_loc[micro_idx * micro:(micro_idx + 1) * micro]
            part_up, part_down = projected_grads(x_micro, dh_micro, w_up, w_down, proj_up, proj_down)
            sum_up = lax.psum_scatter(part_up, 'data', scatter_dimension=2, tiled=True)
            sum_down = lax.psum_scatter(part_down, 'data', scatter_dimension=1, tiled=True)
            scattered.append((sum_up, sum_down))
        red_up = scattered[0][0] + scattered[1][0]
        red_down = scattered[0][1] + scattered[1][1]
        new_mom_up, new_var_up, dir_up = adam_shard(mom_up, var_up, red_up)
        new_mom_down, new_var_down, dir_down = adam_shard(mom_down, var_down, red_down)
        shard_cols = mom_up.shape[2]
        col_start = lax.axis_index('data') * shard_cols
        w_up_loc = lax.dynamic_slice_in_dim(w_up, col_start, shard_cols, axis=2)
        w_down_loc = lax.dynamic_slice_in_dim(w_down, col_start, shard_cols, axis=1)
        delta_up = jnp.einsum('ldr,lrf->ldf', proj_up, dir_up, preferred_element_type=jnp.float32)
        delta_down = jnp.einsum('lfr,ldr->lfd', dir_down, proj_down, preferred_element_type=jnp.float32)
        new_up_loc = (w_up_loc - (LEARN_RATE * ALPHA_SCALE) * delta_up).astype(jnp.bfloat16)
        new_down_loc = (w_down_loc - (LEARN_RATE * ALPHA_SCALE) * delta_down).astype(jnp.bfloat16)
        new_w_up = lax.all_gather(new_up_loc, 'data', axis=2, tiled=True)
        new_w_down = lax.all_gather(new_down_loc, 'data', axis=1, tiled=True)
        return new_w_up, new_w_down, new_mom_up, new_var_up, new_mom_down, new_var_down

    tok_spec = P('data', None)
    up_spec = P(None, None, 'data')
    down_spec = P(None, 'data', None)
    return jax.shard_map(
        local_step,
        mesh=mesh,
        in_specs=(tok_spec, tok_spec, P(), P(), P(), P(), up_spec, up_spec, down_spec, down_spec),
        out_specs=(P(), P(), up_spec, up_spec, down_spec, down_spec),
        check_vma=False,
    )
```

profile of v0, /device:TPU:0, one launch (start us, length us, event | category | flops | bytes accessed | tf_op | source)
XLA Modules:
  0.0 1868.4 jit_solution(840066689984462339)
XLA Ops:
  7.2 0.0 all-reduce.3.cloned.1.call-start
  7.2 0.0 copy-start.4
  7.2 0.0 copy-start.5
  7.2 10.0 fusion.105
  17.2 0.0 copy-done.4
  17.2 0.6 copy-done.5
  17.8 6.1 fusion.97
  23.9 53.5 %fusion.50 = f32[2048,5632]{1,0:T(8,128)} fusion(bf16[2,2048,5632]{2,1,0:T(8,128)(2,1)} %param.12, bf16[4096,2048]{1,0:T(8,128)(2,1)S(1)} %copy-done.4), kind=kOutput, calls=%fused_computation.60 | convolution fusion | flops 47244640256 | bytes 77594624 | tf_op jit(solution)/shard_map/dot_general | solution.py:28
  77.5 53.6 %fusion.48 = f32[2048,5632]{1,0:T(8,128)} fusion(bf16[2,2048,5632]{2,1,0:T(8,128)(2,1)} %param.12, bf16[4096,2048]{1,0:T(8,128)(2,1)S(1)} %copy-done.4), kind=kOutput, calls=%fused_computation.58 | convolution fusion | flops 47244640256 | bytes 77594624 | tf_op jit(solution)/shard_map/dot_general | solution.py:28
  131.1 66.4 %add_convert_fusion.1 = bf16[2048,2048]{1,0:T(8,128)(2,1)} fusion(bf16[2,5632,2048]{2,1,0:T(8,128)(2,1)} %param.13, bf16[4096,2048]{1,0:T(8,128)(2,1)} %param.10, f32[2048,5632]{1,0:T(8,128)} %fusion.48), kind=kOutput, calls=%fused_computation.73 | convolution fusion | flops 47361032192 | bytes 85983232 | tf_op jit(solution)/shard_map/dot_general | solution.py:31
  197.5 56.0 %fusion.30 = f32[2048,5632]{1,0:T(8,128)} fusion(bf16[2048,2048]{1,0:T(8,128)(2,1)} %add_convert_fusion.1, bf16[2,2048,5632]{2,1,0:T(8,128)(2,1)} %param.12), kind=kOutput, calls=%fused_computation.44 | convolution fusion | flops 47244640256 | bytes 77594624 | tf_op jit(solution)/shard_map/dot_general | solution.py:28
  253.5 93.2 %fusion.27 = bf16[2048,5632]{1,0:T(8,128)(2,1)} fusion(f32[2048,5632]{1,0:T(8,128)} %fusion.30, bf16[2,5632,2048]{2,1,0:T(8,128)(2,1)} %param.13, bf16[4096,2048]{1,0:T(8,128)(2,1)} %param.11), kind=kOutput, calls=%fused_computation.35 | convolution fusion | flops 47475326976 | bytes 100663296 | tf_op jit(solution)/shard_map/dot_general | solution.py:19
  346.7 31.6 %convolution_bitcast_fusion = f32[1,512,5632]{2,1,0:T(8,128)} fusion(bf16[2048,5632]{1,0:T(8,128)(2,1)} %fusion.27, bf16[2048,2048]{1,0:T(8,128)(2,1)} %add_convert_fusion.1, bf16[2,2048,512]{2,1,0:T(8,128)(2,1)} %param.14), kind=kOutput, calls=%fused_computation.87 | convolution fusion | flops 16107175936 | bytes 45088768 | tf_op jit(solution)/shard_map/dot_general | solution.py:15
  378.2 62.4 %add_convert_fusion = bf16[2048,2048]{1,0:T(8,128)(2,1)} fusion(bf16[2048,5632]{1,0:T(8,128)(2,1)} %fusion.27, bf16[2,2048,5632]{2,1,0:T(8,128)(2,1)} %param.12, bf16[4096,2048]{1,0:T(8,128)(2,1)} %param.11), kind=kOutput, calls=%fused_computation.72 | convolution fusion | flops 47257223168 | bytes 62914560 | tf_op jit(solution)/shard_map/dot_general | solution.py:19
  440.7 66.4 %add_convert_fusion.3 = bf16[2048,2048]{1,0:T(8,128)(2,1)} fusion(bf16[2,5632,2048]{2,1,0:T(8,128)(2,1)} %param.13, bf16[4096,2048]{1,0:T(8,128)(2,1)} %param.10, f32[2048,5632]{1,0:T(8,128)} %fusion.50), kind=kOutput, calls=%fused_computation.75 | convolution fusion | flops 47361032192 | bytes 85983232 | tf_op jit(solution)/shard_map/dot_general | solution.py:31
  507.1 56.0 %fusion.34 = f32[2048,5632]{1,0:T(8,128)} fusion(bf16[2048,2048]{1,0:T(8,128)(2,1)} %add_convert_fusion.3, bf16[2,2048,5632]{2,1,0:T(8,128)(2,1)} %param.12), kind=kOutput, calls=%fused_computation.48 | convolution fusion | flops 47244640256 | bytes 77594624 | tf_op jit(solution)/shard_map/dot_general | solution.py:28
  563.0 93.3 %fusion.13 = bf16[2048,5632]{1,0:T(8,128)(2,1)} fusion(f32[2048,5632]{1,0:T(8,128)} %fusion.34, bf16[2,5632,2048]{2,1,0:T(8,128)(2,1)} %param.13, bf16[4096,2048]{1,0:T(8,128)(2,1)} %param.11), kind=kOutput, calls=%fused_computation.21 | convolution fusion | flops 47475326976 | bytes 100663296 | tf_op jit(solution)/shard_map/dot_general | solution.py:19
  656.3 31.9 %convolution_bitcast_fusion.2 = f32[1,512,5632]{2,1,0:T(8,128)} fusion(bf16[2048,5632]{1,0:T(8,128)(2,1)} %fusion.13, bf16[2048,2048]{1,0:T(8,128)(2,1)} %add_convert_fusion.3, bf16[2,2048,512]{2,1,0:T(8,128)(2,1)} %param.14), kind=kOutput, calls=%fused_computation.89 | convolution fusion | flops 16107175936 | bytes 45088768 | tf_op jit(solution)/shard_map/dot_general | solution.py:15
  688.2 62.4 %add_convert_fusion.2 = bf16[2048,2048]{1,0:T(8,128)(2,1)} fusion(bf16[2048,5632]{1,0:T(8,128)(2,1)} %fusion.13, bf16[2,2048,5632]{2,1,0:T(8,128)(2,1)} %param.12, bf16[4096,2048]{1,0:T(8,128)(2,1)} %param.11), kind=kOutput, calls=%fused_computation.74 | convolution fusion | flops 47257223168 | bytes 62914560 | tf_op jit(solution)/shard_map/dot_general | solution.py:19
  750.6 91.4 %convolution_bitcast_fusion.1 = f32[1,512,5632]{2,1,0:T(8,128)} fusion(bf16[2048,512]{1,0:T(8,128)(2,1)} %fusion.105, f32[2048,5632]{1,0:T(8,128)} %fusion.48, bf16[2048,2048]{1,0:T(8,128)(2,1)} %add_convert_fusion, bf16[2,5632,2048]{2,1,0:T(8,128)(2,1)} %param.13), kind=kOutput, calls=%fused_computation.88 | convolution fusion | flops 59286487040 | bytes 91226112 | tf_op jit(solution)/shard_map/dot_general | solution.py:15
  842.1 0.0 copy-done.7
  842.1 91.0 %convolution_bitcast_fusion.3 = f32[1,512,5632]{2,1,0:T(8,128)} fusion(bf16[2048,512]{1,0:T(8,128)(2,1)S(1)} %copy-done.7, f32[2048,5632]{1,0:T(8,128)} %fusion.50, bf16[2048,2048]{1,0:T(8,128)(2,1)} %add_convert_fusion.2, bf16[2,5632,2048]{2,1,0:T(8,128)(2,1)} %param.13), kind=kOutput, calls=%fused_computation.90 | convolution fusion | flops 59286487040 | bytes 91226112 | tf_op jit(solution)/shard_map/dot_general | solution.py:15
  933.1 23.5 %maximum_add_fusion = f32[2,512,5632]{2,1,0:T(8,128)} fusion(f32[1,512,5632]{2,1,0:T(8,128)} %convolution_bitcast_fusion.2, f32[1,512,5632]{2,1,0:T(8,128)} %convolution_bitcast_fusion.3, f32[1,512,5632]{2,1,0:T(8,128)} %convolution_bitcast_fusion, f32[1,512,5632]{2,1,0:T(8,128)} %convolution_bitcast_fusion.1), kind=kLoop, calls=%fused_computation.40 | loop fusion | flops 17301504 | bytes 69206016 | tf_op jit(solution)/shard_map/add | solution.py:70
  956.6 33.9 %copy.32 = f32[2,512,5632]{1,0,2:T(2,128)} copy(f32[2,512,5632]{2,1,0:T(8,128)} %maximum_add_fusion) | data formatting | bytes 46137344 | tf_op jit(solution)/shard_map/add | solution.py:70
  990.6 0.0 all-reduce.3.cloned.1.call-update
  990.6 0.0 reduce-scatter.2.cloned.1.call-start
  990.6 0.0 copy-start.6
  990.7 0.0 slice-start
  990.7 10.0 fusion.108.clone.5
  1000.6 0.0 copy-done.6
  1000.6 8.5 fusion.100.clone.5
  1009.1 0.0 slice-done
  1009.1 0.0 slice-done.1
  1009.1 5.9 convolution_convert_fusion.clone.5
  1015.1 29.3 %fusion.75 = f32[1,5632,512]{2,1,0:T(8,128)} fusion(f32[2048,5632]{1,0:T(8,128)} %fusion.30, bf16[2048,512]{1,0:T(8,128)(2,1)} %fusion.108.clone.5), kind=kOutput, calls=%fused_computation.93 | convolution fusion | flops 11914969088 | bytes 59768832 | tf_op jit(solution)/shard_map/dot_general | solution.py:15
  1044.4 29.6 %convolution_bitcast_fusion.4 = f32[1,5632,512]{2,1,0:T(8,128)} fusion(f32[2048,5632]{1,0:T(8,128)} %fusion.48, bf16[2048,512]{1,0:T(8,128)(2,1)} %convolution_convert_fusion.clone.5), kind=kOutput, calls=%fused_computation.91 | convolution fusion | flops 11914969088 | bytes 59768832 | tf_op jit(solution)/shard_map/dot_general | solution.py:15
  1074.0 9.1 convolution_convert_fusion.1.clone.2
  1083.0 0.0 copy-start.8
  1083.0 29.1 %fusion.76 = f32[1,5632,512]{2,1,0:T(8,128)} fusion(f32[2048,5632]{1,0:T(8,128)} %fusion.34, bf16[2048,512]{1,0:T(8,128)(2,1)S(1)} %fusion.100.clone.5), kind=kOutput, calls=%fused_computation.94 | convolution fusion | flops 11914969088 | bytes 59768832 | tf_op jit(solution)/shard_map/dot_general | solution.py:15
  1112.1 0.0 copy-done.8
  1112.1 28.8 %convolution_bitcast_fusion.5 = f32[1,5632,512]{2,1,0:T(8,128)} fusion(f32[2048,5632]{1,0:T(8,128)} %fusion.50, bf16[2048,512]{1,0:T(8,128)(2,1)S(1)} %copy-done.8), kind=kOutput, calls=%fused_computation.92 | convolution fusion | flops 11914969088 | bytes 59768832 | tf_op jit(solution)/shard_map/dot_general | solution.py:15
  1141.0 23.7 %maximum_add_fusion.1 = f32[2,5632,512]{2,1,0:T(8,128)} fusion(f32[1,5632,512]{2,1,0:T(8,128)} %fusion.76, f32[1,5632,512]{2,1,0:T(8,128)} %convolution_bitcast_fusion.5, f32[1,5632,512]{2,1,0:T(8,128)} %fusion.75, f32[1,5632,512]{2,1,0:T(8,128)} %convolution_bitcast_fusion.4), kind=kLoop, calls=%fused_computation.41 | loop fusion | flops 17301504 | bytes 69206016 | tf_op jit(solution)/shard_map/add | solution.py:71
  1164.6 0.0 reduce-scatter.2.cloned.1.call-update
  1164.7 0.0 all-gather.3.cloned.1.call-start
  1164.7 9.8 constant_dynamic-slice_fusion.1
  1174.5 8.4 copy.37
  1182.9 85.1 %all-reduce.3.cloned.1.call-done = f32[2,512,5632]{1,0,2:T(2,128)} async-done(((f32[2,512,5632]{1,0,2:T(2,128)}), f32[2,512,5632]{1,0,2:T(2,128)}) %all-reduce.3.cloned.1.call-update) | async-done | bytes 23068688
  1268.0 2.8 constant_dynamic-slice_fusion
  1270.8 0.0 copy-done
  1270.8 4.7 multiply_add_fusion.1
  1275.5 1.6 copy-done.2
  1277.1 11.7 fusion.74
  1288.8 0.0 all-gather.3.cloned.1.call-update
  1288.8 0.3 all-gather.5.cloned.1.call-start
  1289.1 119.7 %reduce-scatter.2.cloned.1.call-done = f32[2,704,512]{2,1,0:T(8,128)} async-done(((f32[2,5632,512]{2,1,0:T(8,128)}), f32[2,704,512]{2,1,0:T(8,128)}) %reduce-scatter.2.cloned.1.call-update) | async-done | bytes 2883600 | tf_op jit(solution)/shard_map/reduce_scatter | solution.py:68
  1408.8 0.0 copy-done.1
  1408.8 5.4 multiply_add_fusion
  1414.2 1.6 copy-done.3
  1415.7 11.4 subtract_convert_fusion
  1427.1 0.0 all-gather.5.cloned.1.call-update
  1427.1 192.7 %all-gather.3.cloned.1.call-done = bf16[2,2048,5632]{1,2,0:T(8,128)(2,1)} async-done(((bf16[2,2048,704]{1,2,0:T(8,128)(2,1)}), bf16[2,2048,5632]{1,2,0:T(8,128)(2,1)}) %all-gather.3.cloned.1.call-update) | async-done | bytes 46137360 | tf_op jit(solution)/shard_map/all_gather | solution.py:82
  1619.9 55.1 %copy.36 = bf16[2,2048,5632]{2,1,0:T(8,128)(2,1)} copy(bf16[2,2048,5632]{1,2,0:T(8,128)(2,1)} %all-gather.3.cloned.1.call-done) | data formatting | bytes 92274688
  1674.9 155.9 %all-gather.5.cloned.1.call-done = bf16[2,5632,2048]{2,1,0:T(8,128)(2,1)} async-done(((bf16[2,704,2048]{2,1,0:T(8,128)(2,1)}), bf16[2,5632,2048]{2,1,0:T(8,128)(2,1)}) %all-gather.5.cloned.1.call-update) | async-done | bytes 46137360 | tf_op jit(solution)/shard_map/all_gather | solution.py:83
  1830.8 30.8 %copy.42 = bf16[2,5632,2048]{2,1,0:T(8,128)(2,1)} copy(bf16[2,5632,2048]{2,1,0:T(8,128)(2,1)} %all-gather.5.cloned.1.call-done) | data formatting | bytes 92274688
  (7 shorter events, 0.0 us)
Async XLA Ops:
  7.2 1260.8 %all-reduce.3.cloned.1.call-start = ((), (), s32[]{:S(2)}) async-start(), calls=%async_computation.4 | async-start | bytes 46137344
  7.2 10.0 copy-start.4
  7.2 10.6 copy-start.5
  750.6 91.4 %copy-start.7 = (bf16[2048,512]{1,0:T(8,128)(2,1)S(1)}, bf16[2048,512]{1,0:T(8,128)(2,1)}, u32[]{:S(2)}) copy-start(bf16[2048,512]{1,0:T(8,128)(2,1)} %fusion.97) | copy-start | bytes 6291460
  990.6 418.2 %reduce-scatter.2.cloned.1.call-start = ((), (), s32[]{:S(2)}) async-start(), calls=%async_computation.3 | async-start | bytes 25952256 | tf_op jit(solution)/shard_map/reduce_scatter | solution.py:68
  990.6 10.0 copy-start.6
  990.7 18.5 slice-start
  1000.6 8.5 slice-start.1
  1083.0 29.1 %copy-start.8 = (bf16[2048,512]{1,0:T(8,128)(2,1)S(1)}, bf16[2048,512]{1,0:T(8,128)(2,1)}, u32[]{:S(2)}) copy-start(bf16[2048,512]{1,0:T(8,128)(2,1)} %convolution_convert_fusion.1.clone.2) | copy-start | bytes 6291460
  1164.6 106.1 %copy-start = (f32[2,512,704]{1,2,0:T(8,128)S(1)}, f32[2,512,704]{1,2,0:T(8,128)}, u32[]{:S(2)}) copy-start(f32[2,512,704]{1,2,0:T(8,128)} %param.16) | copy-start | bytes 8650756
  1164.7 455.2 %all-gather.3.cloned.1.call-start = ((), (), s32[]{:S(2)}) async-start(), calls=%async_computation.1 | async-start | bytes 51904512 | tf_op jit(solution)/shard_map/all_gather | solution.py:82
  1275.5 1.6 copy-start.2
  1275.5 133.3 %copy-start.1 = (f32[2,704,512]{2,1,0:T(8,128)S(1)}, f32[2,704,512]{2,1,0:T(8,128)}, u32[]{:S(2)}) copy-start(f32[2,704,512]{2,1,0:T(8,128)} %param.18) | copy-start | bytes 8650756
  1288.8 541.9 %all-gather.5.cloned.1.call-start = ((), (), s32[]{:S(2)}) async-start(), calls=%async_computation.2 | async-start | bytes 51904512 | tf_op jit(solution)/shard_map/all_gather | solution.py:83
  1414.2 1.6 copy-start.3
Sparse Core Ops, SparseCore 0:
  990.7 277.1 all-reduce.2
  1272.1 136.6 reduce-scatter.1
  1411.2 208.5 all-gather.2
  1622.1 208.5 all-gather.4
where the time goes:
time: 1870 us
  matrix products  1100 us (59%)
  waiting for transfers between devices  553 us (30%)
  local copies, waits for them, and re-layouts  145 us (8%)
  other arithmetic  57.3 us (3%)
    dot_general x8, matrix products, contract_rows(): lax.dot_general(lhs, rhs, (((0,), (0,)), ((), ())), preferred_element_typ...  363 us
    dot_general x4, matrix products, contract_cols(): lax.dot_general(lhs, rhs, (((1,), (1,)), ((), ())), preferred_element_typ...  311 us
    dot_general x4, matrix products, projected_grads(): jnp.dot(hidden[layer_idx], w_up[layer_idx], preferred_element_type=jnp.fl...  219 us
    all_gather x1, waiting for transfers between devices, local_step(): new_w_up = lax.all_gather(new_up_loc, 'data', axis=2, tiled=True)  193 us
    all_gather x1, waiting for transfers between devices, local_step(): new_w_down = lax.all_gather(new_down_loc, 'data', axis=1, tiled=True)  156 us
    dot_general x2, matrix products, projected_grads(): jnp.dot(act_val, w_down[layer_idx], preferred_element_type=jnp.float32)  133 us
    reduce_scatter x1, waiting for transfers between devices, local_step(): lax.psum_scatter(part_down, 'data', scatter_dimension=1, tiled=True)  120 us
    unnamed x26, local copies, waits for them, and re-layouts  101 us
  transfers between devices with their start and end apart: 4, of which 4 were waited for; matrix products, arithmetic and copies ran while one was open for 15% of the time, Pallas kernels for 0%

commit v1 on v0

v1 whole, which is shorter than its diff:
```python
import jax
import jax.numpy as jnp
from jax import lax
from jax.experimental import pallas as pl
from jax.experimental.pallas import tpu as pltpu
from jax.sharding import PartitionSpec as P


BETA_ONE = 0.9
BETA_TWO = 0.999
EPSILON = 1e-8
STEP = 4
LEARN_RATE = 0.02
ALPHA_SCALE = 0.25
GELU_C = 0.7978845608028654
GELU_A = 0.044715
VMEM_BYTES = 67_000_000
BF16 = jnp.bfloat16
F32 = jnp.float32


def dot_nn(lhs, rhs):
    return jnp.dot(lhs, rhs, preferred_element_type=F32)


def dot_tn(lhs, rhs):
    return lax.dot_general(lhs, rhs, (((0,), (0,)), ((), ())), preferred_element_type=F32)


def dot_nt(lhs, rhs):
    return lax.dot_general(lhs, rhs, (((1,), (1,)), ((), ())), preferred_element_type=F32)


def gelu_parts(z):
    sq = z * z
    s = 0.5 * jnp.tanh(z * (GELU_C + (GELU_C * GELU_A) * sq)) + 0.5
    g = z * s
    d = s + g * (1.0 - s) * (2.0 * GELU_C + (6.0 * GELU_C * GELU_A) * sq)
    return g, d


def call(body, grid, in_specs, out_specs, out_shape, flops, aliases=None):
    return pl.pallas_call(
        body, grid=grid, in_specs=in_specs, out_specs=out_specs, out_shape=out_shape,
        input_output_aliases=aliases or {},
        cost_estimate=pl.CostEstimate(flops=flops, bytes_accessed=flops // 500, transcendentals=0),
        compiler_params=pltpu.CompilerParams(vmem_limit_bytes=VMEM_BYTES))


def layer_one(h, dh, w_up, w_down, proj_up, proj_down):
    rows, d = h.shape
    ff = w_up.shape[2]
    rank = proj_up.shape[2]
    bm, bn = 1024, 512

    def body(h_ref, dh_ref, up_ref, down_ref, p_ref, q_ref, act_ref, dz_ref, u_ref, v_ref):
        @pl.when(pl.program_id(1) == 0)
        def _():
            u_ref[...] = dot_nn(h_ref[...], p_ref[0]).astype(BF16)
            v_ref[...] = dot_nn(dh_ref[...], q_ref[0]).astype(BF16)

        z = dot_nn(h_ref[...], up_ref[0])
        da = dot_nt(dh_ref[...], down_ref[0])
        g, dg = gelu_parts(z)
        act_ref[...] = g.astype(BF16)
        dz_ref[...] = (dg * da).astype(BF16)

    return call(
        body, (rows // bm, ff // bn),
        [pl.BlockSpec((bm, d), lambda i, j: (i, 0)), pl.BlockSpec((bm, d), lambda i, j: (i, 0)),
         pl.BlockSpec((1, d, bn), lambda i, j: (1, 0, j)), pl.BlockSpec((1, bn, d), lambda i, j: (1, j, 0)),
         pl.BlockSpec((1, d, rank), lambda i, j: (1, 0, 0)), pl.BlockSpec((1, d, rank), lambda i, j: (1, 0, 0))],
        [pl.BlockSpec((bm, bn), lambda i, j: (i, j))] * 2 + [pl.BlockSpec((bm, rank), lambda i, j: (i, 0))] * 2,
        [jax.ShapeDtypeStruct((rows, ff), BF16)] * 2 + [jax.ShapeDtypeStruct((rows, rank), BF16)] * 2,
        4 * rows * d * (ff + rank))(h, dh, w_up, w_down, proj_up, proj_down)


def project_pair(act, v, dz, u):
    rows, ff = act.shape
    rank = v.shape[1]
    bn = 512

    def body(act_ref, v_ref, dz_ref, u_ref, out_ref):
        out_ref[:, :rank] = dot_tn(act_ref[...], v_ref[...])
        out_ref[:, rank:] = dot_tn(dz_ref[...], u_ref[...])

    col = pl.BlockSpec((rows, bn), lambda j: (0, j))
    full = pl.BlockSpec((rows, rank), lambda j: (0, 0))
    return call(body, (ff // bn,), [col, full, col, full], pl.BlockSpec((bn, 2 * rank), lambda j: (j, 0)),
                jax.ShapeDtypeStruct((ff, 2 * rank), F32), 4 * rows * ff * rank)(act, v, dz, u)


def layer_zero_forward(x, w_up, proj_up):
    rows, d = x.shape
    ff = w_up.shape[2]
    rank = proj_up.shape[2]
    bm, bn = 2048, 512

    def body(x_ref, up_ref, p_ref, act_ref, slope_ref, u_ref):
        g, dg = gelu_parts(dot_nn(x_ref[...], up_ref[0]))
        act_ref[...] = g.astype(BF16)
        slope_ref[...] = dg

        @pl.when(pl.program_id(1) == 0)
        def _():
            u_ref[...] = dot_nn(x_ref[...], p_ref[0]).astype(BF16)

    return call(
        body, (rows // bm, ff // bn),
        [pl.BlockSpec((bm, d), lambda i, j: (i, 0)), pl.BlockSpec((1, d, bn), lambda i, j: (0, 0, j)),
         pl.BlockSpec((1, d, rank), lambda i, j: (0, 0, 0))],
        [pl.BlockSpec((bm, bn), lambda i, j: (i, j))] * 2 + [pl.BlockSpec((bm, rank), lambda i, j: (i, 0))],
        [jax.ShapeDtypeStruct((rows, ff), BF16), jax.ShapeDtypeStruct((rows, ff), F32),
         jax.ShapeDtypeStruct((rows, rank), BF16)],
        2 * rows * d * (ff + rank))(x, w_up, proj_up)


def project_one(act, v, order):
    rows, ff = act.shape
    rank = v.shape[1]
    bn = 512

    def body(act_ref, v_ref, *rest):
        rest[-1][...] = dot_tn(act_ref[...], v_ref[...])

    return call(body, (ff // bn,),
                [pl.BlockSpec((rows, bn), lambda j: (0, j)), pl.BlockSpec((rows, rank), lambda j: (0, 0))]
                + [pl.BlockSpec(memory_space=pl.ANY)] * len(order),
                pl.BlockSpec((bn, rank), lambda j: (j, 0)),
                jax.ShapeDtypeStruct((ff, rank), F32), 2 * rows * ff * rank)(act, v, *order)


def layer_zero_backward(g1, u, w_down, slope, first, count, old, order):
    rows, d = g1.shape
    ff = slope.shape[1]
    rank = u.shape[1]
    bm, bn = 2048, 512

    def body(g_ref, u_ref, down_ref, slope_ref, *rest):
        out_ref = rest[-1]
        i = pl.program_id(1)
        dz = (slope_ref[...] * dot_nt(g_ref[...], down_ref[0])).astype(BF16)
        part = dot_tn(dz, u_ref[...])

        @pl.when(i == 0)
        def _():
            out_ref[...] = part

        @pl.when(i > 0)
        def _():
            out_ref[...] += part

    extra = list(old) + list(order)
    return call(
        body, (count, rows // bm),
        [pl.BlockSpec((bm, d), lambda j, i: (i, 0)), pl.BlockSpec((bm, rank), lambda j, i: (i, 0)),
         pl.BlockSpec((1, bn, d), lambda j, i: (0, j + first, 0)),
         pl.BlockSpec((bm, bn), lambda j, i: (i, j + first))]
        + [pl.BlockSpec(memory_space=pl.ANY)] * len(extra),
        pl.BlockSpec((bn, rank), lambda j, i: (j + first, 0)),
        jax.ShapeDtypeStruct((ff, rank), F32),
        2 * rows * count * bn * (d + rank), aliases={4: 0} if old else None)(
            g1, u, w_down, slope, *extra)


def update_up(layer, w_up, proj_up, dirs, at, old, order):
    d, ff = w_up.shape[1:]
    rank = proj_up.shape[2]
    bn = 512
    scale = LEARN_RATE * ALPHA_SCALE

    def body(up_ref, p_ref, dir_ref, *rest):
        rest[-1][0] = (up_ref[0] - scale * dot_nt(p_ref[0], dir_ref[...])).astype(BF16)

    extra = list(old) + list(order)
    block = pl.BlockSpec((1, d, bn), lambda j: (layer, 0, j))
    return call(body, (ff // bn,),
                [block, pl.BlockSpec((1, d, rank), lambda j: (layer, 0, 0)),
                 pl.BlockSpec((bn, rank), lambda j: (j, at))] + [pl.BlockSpec(memory_space=pl.ANY)] * len(extra),
                block, jax.ShapeDtypeStruct(w_up.shape, BF16), 2 * d * ff * rank,
                aliases={3: 0} if old else None)(w_up, proj_up, dirs, *extra)


def update_down(layer, w_down, proj_down, dirs, at, old, order):
    ff, d = w_down.shape[1:]
    rank = proj_down.shape[2]
    bn = 512
    scale = LEARN_RATE * ALPHA_SCALE

    def body(down_ref, q_ref, dir_ref, *rest):
        rest[-1][0] = (down_ref[0] - scale * dot_nt(dir_ref[...], q_ref[0])).astype(BF16)

    extra = list(old) + list(order)
    block = pl.BlockSpec((1, bn, d), lambda j: (layer, j, 0))
    return call(body, (ff // bn,),
                [block, pl.BlockSpec((1, d, rank), lambda j: (layer, 0, 0)),
                 pl.BlockSpec((bn, rank), lambda j: (j, at))] + [pl.BlockSpec(memory_space=pl.ANY)] * len(extra),
                block, jax.ShapeDtypeStruct(w_down.shape, BF16), 2 * d * ff * rank,
                aliases={3: 0} if old else None)(w_down, proj_down, dirs, *extra)


def adam(moment, variance, grad_red):
    new_mom = BETA_ONE * moment + (1.0 - BETA_ONE) * grad_red
    new_var = BETA_TWO * variance + (1.0 - BETA_TWO) * grad_red * grad_red
    bias_one = 1.0 - BETA_ONE ** STEP
    bias_two = 1.0 - BETA_TWO ** STEP
    direction = (new_mom / bias_one) / (jnp.sqrt(new_var / bias_two) + EPSILON)
    return new_mom, new_var, direction.astype(BF16)


def solution(mesh):
    def local_step(x, dh, w_up, w_down, proj_up, proj_down, mom_up, var_up, mom_down, var_down):
        rank = proj_up.shape[2]

        def scatter(part):
            return lax.psum_scatter(part, 'data', scatter_dimension=0, tiled=True)

        def gather(part):
            return lax.all_gather(part, 'data', axis=0, tiled=True)

        a0, slope0, u0 = layer_zero_forward(x, w_up, proj_up)
        h1 = (x + dot_nn(a0, w_down[0])).astype(BF16)
        a1, dz1, u1, v1 = layer_one(h1, dh, w_up, w_down, proj_up, proj_down)
        red1 = scatter(project_pair(a1, v1, dz1, u1))
        g1 = (dh + dot_nt(dz1, w_up[1])).astype(BF16)
        v0 = dot_nn(g1, proj_down[0]).astype(BF16)

        down1 = adam(mom_down[1], var_down[1], red1[:, :rank])
        up1 = adam(mom_up[1].T, var_up[1].T, red1[:, rank:])
        dir1 = jnp.concatenate([down1[2], up1[2]], axis=1)
        dirs1 = gather(dir1)

        down0 = adam(mom_down[0], var_down[0], scatter(project_one(a0, v0, (dir1,))))
        dirs_down0 = gather(down0[2])
        blocks = w_up.shape[2] // 512
        part = layer_zero_backward(g1, u0, w_down, slope0, 0, blocks - 2, (), ())
        part = layer_zero_backward(g1, u0, w_down, slope0, blocks - 2, 2, (part,), (down0[2],))
        up0 = adam(mom_up[0].T, var_up[0].T, scatter(part))
        dirs_up0 = gather(up0[2])

        new_up = update_up(1, w_up, proj_up, dirs1, 1, (), (part,))
        new_down = update_down(1, w_down, proj_down, dirs1, 0, (), (part,))
        new_down = update_down(0, w_down, proj_down, dirs_down0, 0, (new_down,), ())
        new_up = update_up(0, w_up, proj_up, dirs_up0, 0, (new_up,), ())
        return (new_up, new_down, jnp.stack([up0[0].T, up1[0].T]), jnp.stack([up0[1].T, up1[1].T]),
                jnp.stack([down0[0], down1[0]]), jnp.stack([down0[1], down1[1]]))

    tok_spec = P('data', None)
    up_spec = P(None, None, 'data')
    down_spec = P(None, 'data', None)
    return jax.shard_map(
        local_step,
        mesh=mesh,
        in_specs=(tok_spec, tok_spec, P(), P(), P(), P(), up_spec, up_spec, down_spec, down_spec),
        out_specs=(P(), P(), up_spec, up_spec, down_spec, down_spec),
        check_vma=False,
    )
```

time: 1870 us -> 1160 us (0.62)
  matrix products: 1100 us -> 232 us
  Pallas kernels: 0 us -> 731 us
  waiting for transfers between devices: 553 us -> 147 us
  local copies, waits for them, and re-layouts: 145 us -> 0.01 us
  other arithmetic: 57.3 us -> 30.5 us
    dot_general x26 -> x3, matrix products: 1100 us -> 232 us  [the longest x2 121 us: dot_nn(): return jnp.dot(lhs, rhs, preferred_element_type=F32)]
    pallas_call x0 -> x10, Pallas kernels: none -> 731 us  [the longest x1 231 us: layer_one(): call(body, (rows // bm, ff // bn), [pl.BlockSpec((bm, d), lambda i, j: (i...]
    all_gather x2 -> x3, waiting for transfers between devices: 349 us -> 52.7 us  [gather(): return lax.all_gather(part, 'data', axis=0, tiled=True)]
    unnamed x26 -> x6, local copies, waits for them, and re-layouts: 101 us -> 0.01 us
    unnamed x5 -> x6, waiting for transfers between devices: 85.1 us -> 1.12 us
    add x4 -> x0, other arithmetic: 57.3 us -> none  [the longest x1 23.7 us: local_step(): red_down = scattered[0][1] + scattered[1][1]]
    add x1 -> x0, local copies, waits for them, and re-layouts: 33.9 us -> none  [local_step(): red_up = scattered[0][0] + scattered[1][0]]
    another operation x0 -> x5, other arithmetic: none -> 29.2 us  [the longest x2 12.4 us: local_step(): jnp.stack([down0[1], down1[1]])]
  transfers between devices with their start and end apart: 4 -> 6, of which waited for: 4 -> 3; matrix products, arithmetic and copies ran while one was open for 15% -> 12% of each run, Pallas kernels for 0% -> 17%
where the time goes in v1:
time: 1160 us; the launch traced here: 1150 us
  Pallas kernels  731 us (63%)
  matrix products  232 us (20%)
  waiting for transfers between devices  147 us (13%)
  other arithmetic  30.5 us (3%)
  between operations  14.3 us (1%)
    pallas_call x1, Pallas kernels, layer_one(): call(body, (rows // bm, ff // bn), [pl.BlockSpec((bm, d), lambda i, j: (i...  231 us
    pallas_call x1, Pallas kernels, layer_zero_forward(): call(body, (rows // bm, ff // bn), [pl.BlockSpec((bm, d), lambda i, j: (i...  156 us
    pallas_call x2, Pallas kernels, layer_zero_backward(): call(body, (count, rows // bm), [pl.BlockSpec((bm, d), lambda j, i: (i, 0...  147 us
    dot_general x2, matrix products, dot_nn(): return jnp.dot(lhs, rhs, preferred_element_type=F32)  121 us
    dot_general x1, matrix products, dot_nt(): lax.dot_general(lhs, rhs, (((1,), (1,)), ((), ())), preferred_element_typ...  111 us
    reduce_scatter x3, waiting for transfers between devices, scatter(): return lax.psum_scatter(part, 'data', scatter_dimension=0, tiled=True)  93 us
    pallas_call x1, Pallas kernels, project_pair(): call(body, (ff // bn,), [col, full, col, full], pl.BlockSpec((bn, 2 * ran...  57.2 us
    pallas_call x2, Pallas kernels, update_up(): call(body, (ff // bn,), [block, pl.BlockSpec((1, d, rank), lambda j: (lay...  54.6 us
  transfers between devices with their start and end apart: 6, of which 3 were waited for; matrix products, arithmetic and copies ran while one was open for 12% of the time, Pallas kernels for 17%

profile of v1, /device:TPU:0, one launch (start us, length us, event | category | flops | bytes accessed | tf_op | source)
XLA Modules:
  0.0 1154.6 jit_solution(8851563369028201398)
XLA Ops:
  7.2 0.0 reduce-scatter.4.cloned.1.call-start
  7.2 156.3 %shard_map.145 = (bf16[4096,5632]{1,0:T(8,128)(2,1)}, f32[4096,5632]{1,0:T(8,128)}, bf16[4096,512]{1,0:T(8,128)(2,1)}) custom-call(bf16[4096,2048]{1,0:T(8,128)(2,1)} %x_ref.1, bf16[2,2048,5632]{2,1,0:T(8,128)(2,1)} %up_ref.7, bf16[2,2048,512]{2,1,0:T(8,128)(2,1)} %p_ref.7), custom_call_target="tpu_custom_call" | custom-call | flops 103079215104 | bytes 206158432 | tf_op jit(solution)/shard_map/pallas_call | solution.py:108
  163.5 106.2 %add_convert_fusion.1.h_ref = bf16[4096,2048]{1,0:T(8,128)(2,1)} fusion(bf16[4096,2048]{1,0:T(8,128)(2,1)} %x_ref.1, bf16[4096,5632]{1,0:T(8,128)(2,1)} %get-tuple-element.13.act_ref, bf16[2,5632,2048]{2,1,0:T(8,128)(2,1)} %down_ref.9), kind=kOutput, calls=%fused_computation.1 | convolution fusion | flops 94514446336 | bytes 102760448 | tf_op jit(solution)/shard_map/dot_general | solution.py:23
  269.7 231.1 %shard_map.146 = (bf16[4096,5632]{1,0:T(8,128)(2,1)}, bf16[4096,5632]{1,0:T(8,128)(2,1)}, bf16[4096,512]{1,0:T(8,128)(2,1)}, bf16[4096,512]{1,0:T(8,128)(2,1)}) custom-call(bf16[4096,2048]{1,0:T(8,128)(2,1)} %add_convert_fusion.1.h_ref, bf16[4096,2048]{1,0:T(8,128)(2,1)} %dh_ref.1, bf16[2,2048,5632]{2,1,0:T(8,128)(2,1)} %up_ref.7, ...), custom_call_target="tpu_custom_call" | custom-call | flops 206158430208 | bytes 412316864 | tf_op jit(solution)/shard_map/pallas_call | solution.py:68
  500.8 57.2 %shard_map.148 = f32[5632,1024]{1,0:T(8,128)} custom-call(bf16[4096,5632]{1,0:T(8,128)(2,1)} %get-tuple-element.17.act_ref, bf16[4096,512]{1,0:T(8,128)(2,1)} %get-tuple-element.18.v_ref, bf16[4096,5632]{1,0:T(8,128)(2,1)} %get-tuple-element.14.dz_ref, bf16[4096,512]{1,0:T(8,128)(2,1)} %get-tuple-element.19.u_ref), custom_call_target="tpu_custom_call" | custom-call | flops 47244640256 | bytes 94489280 | tf_op jit(solution)/shard_map/pallas_call | solution.py:89
  558.0 0.0 reduce-scatter.4.cloned.1.call-update
  558.1 0.0 reduce-scatter.6.cloned.1.call-start
  558.1 110.8 %add_convert_fusion.g_ref = bf16[4096,2048]{1,0:T(8,128)(2,1)} fusion(bf16[4096,2048]{1,0:T(8,128)(2,1)} %dh_ref.1, bf16[4096,5632]{1,0:T(8,128)(2,1)} %get-tuple-element.14.dz_ref, bf16[2,2048,5632]{2,1,0:T(8,128)(2,1)} %up_ref.7), kind=kOutput, calls=%fused_computation | convolution fusion | flops 94514446336 | bytes 102760448 | tf_op jit(solution)/shard_map/dot_general | solution.py:31
  668.9 0.0 copy-start.2
  668.9 14.9 %convolution_convert_fusion.v_ref = bf16[4096,512]{1,0:T(8,128)(2,1)} fusion(bf16[4096,2048]{1,0:T(8,128)(2,1)} %add_convert_fusion.g_ref, bf16[2,2048,512]{2,1,0:T(8,128)(2,1)} %q_ref.5), kind=kOutput, calls=%fused_computation.8 | convolution fusion | flops 8592031744 | bytes 23068672 | tf_op jit(solution)/shard_map/dot_general | solution.py:23
  683.8 15.3 %reduce-scatter.4.cloned.1.call-done = f32[704,1024]{1,0:T(8,128)} async-done(((f32[5632,1024]{1,0:T(8,128)}), f32[704,1024]{1,0:T(8,128)}) %reduce-scatter.4.cloned.1.call-update) | async-done | bytes 2883600 | tf_op jit(solution)/shard_map/reduce_scatter | solution.py:216
  699.0 0.0 copy-done.2
  699.0 7.4 fusion.23
  706.4 1.3 pad_maximum_fusion.4.rest_0_
  707.8 31.6 %shard_map.149 = f32[5632,512]{1,0:T(8,128)} custom-call(bf16[4096,5632]{1,0:T(8,128)(2,1)} %get-tuple-element.13.act_ref, bf16[4096,512]{1,0:T(8,128)(2,1)} %convolution_convert_fusion.v_ref, bf16[704,1024]{1,0:T(8,128)(2,1)} %pad_maximum_fusion.4.rest_0_), custom_call_target="tpu_custom_call" | custom-call | flops 23622320128 | bytes 47244640 | tf_op jit(solution)/shard_map/pallas_call | solution.py:126
  739.3 0.0 reduce-scatter.6.cloned.1.call-update
  739.4 0.0 reduce-scatter.8.cloned.1.call-start
  739.4 116.8 %shard_map.147.rest_0_ = f32[5632,512]{1,0:T(8,128)} custom-call(bf16[4096,2048]{1,0:T(8,128)(2,1)} %add_convert_fusion.g_ref, bf16[4096,512]{1,0:T(8,128)(2,1)} %get-tuple-element.15.u_ref, bf16[2,5632,2048]{2,1,0:T(8,128)(2,1)} %down_ref.9, f32[4096,5632]{1,0:T(8,128)} %get-tuple-element.16.slope_ref), custom_call_target="tpu_custom_call" | custom-call | flops 96636764160 | bytes 193273536 | tf_op jit(solution)/shard_map/pallas_call | solution.py:154
  856.2 0.0 reduce-scatter.6.cloned.1.call-done
  856.2 5.0 fusion.21
  861.3 29.9 %shard_map.150.rest_0_ = f32[5632,512]{1,0:T(8,128)} custom-call(bf16[4096,2048]{1,0:T(8,128)(2,1)} %add_convert_fusion.g_ref, bf16[4096,512]{1,0:T(8,128)(2,1)} %get-tuple-element.15.u_ref, bf16[2,5632,2048]{2,1,0:T(8,128)(2,1)} %down_ref.9, f32[4096,5632]{1,0:T(8,128)} %get-tuple-element.16.slope_ref, ...), custom_call_target="tpu_custom_call", output_to_operand_aliasing={{}: (4, {})} | custom-call | flops 21474836480 | bytes 42949672 | tf_op jit(solution)/shard_map/pallas_call | solution.py:154
  891.2 0.0 reduce-scatter.8.cloned.1.call-update
  891.2 0.0 all-gather.6.cloned.1.call-start
  891.2 0.5 all-gather.6.cloned.1.call-update
  891.8 0.0 all-gather.8.cloned.1.call-start
  891.8 0.5 all-gather.8.cloned.1.call-update
  892.4 0.2 all-gather.4.cloned.1.call-start
  892.6 77.7 %reduce-scatter.8.cloned.1.call-done = f32[704,512]{1,0:T(8,128)} async-done(((f32[5632,512]{1,0:T(8,128)}), f32[704,512]{1,0:T(8,128)}) %reduce-scatter.8.cloned.1.call-update) | async-done | bytes 1441808 | tf_op jit(solution)/shard_map/reduce_scatter | solution.py:216
  970.3 0.0 copy-start
  970.3 0.0 copy-start.1
  970.3 5.2 fusion.20
  975.5 0.0 all-gather.4.cloned.1.call-update
  975.5 0.0 copy-done
  975.5 0.0 copy-done.1
  975.6 5.7 pad_maximum_fusion.2
  981.3 52.7 %all-gather.6.cloned.1.call-done.dir_ref = bf16[5632,1024]{1,0:T(8,128)(2,1)} async-done(((bf16[704,1024]{1,0:T(8,128)(2,1)}), bf16[5632,1024]{1,0:T(8,128)(2,1)}) %all-gather.6.cloned.1.call-update) | async-done | bytes 11534352 | tf_op jit(solution)/shard_map/all_gather | solution.py:219
  1034.0 26.3 %shard_map.153.rest_0_ = bf16[2,5632,2048]{2,1,0:T(8,128)(2,1)} custom-call(bf16[2,5632,2048]{2,1,0:T(8,128)(2,1)} %down_ref.9, bf16[2,2048,512]{2,1,0:T(8,128)(2,1)} %q_ref.5, bf16[5632,1024]{1,0:T(8,128)(2,1)} %all-gather.6.cloned.1.call-done.dir_ref, f32[5632,512]{1,0:T(8,128)} %shard_map.150.rest_0_), custom_call_target="tpu_custom_call" | custom-call | flops 11811160064 | bytes 23622320 | tf_op jit(solution)/shard_map/pallas_call | solution.py:195
  1060.3 27.2 %shard_map.151.rest_0_ = bf16[2,2048,5632]{2,1,0:T(8,128)(2,1)} custom-call(bf16[2,2048,5632]{2,1,0:T(8,128)(2,1)} %up_ref.7, bf16[2,2048,512]{2,1,0:T(8,128)(2,1)} %p_ref.7, bf16[5632,1024]{1,0:T(8,128)(2,1)} %all-gather.6.cloned.1.call-done.dir_ref, f32[5632,512]{1,0:T(8,128)} %shard_map.150.rest_0_), custom_call_target="tpu_custom_call" | custom-call | flops 11811160064 | bytes 23622320 | tf_op jit(solution)/shard_map/pallas_call | solution.py:177
  1087.5 0.0 all-gather.8.cloned.1.call-done.dir_ref
  1087.5 26.8 %shard_map.154 = bf16[2,5632,2048]{2,1,0:T(8,128)(2,1)} custom-call(bf16[2,5632,2048]{2,1,0:T(8,128)(2,1)} %down_ref.9, bf16[2,2048,512]{2,1,0:T(8,128)(2,1)} %q_ref.5, bf16[5632,512]{1,0:T(8,128)(2,1)} %all-gather.8.cloned.1.call-done.dir_ref, bf16[2,5632,2048]{2,1,0:T(8,128)(2,1)} %shard_map.153.rest_0_), custom_call_target="tpu_custom_call", output_to_operand_aliasing={{}: (3, {})} | custom-call | flops 11811160064 | bytes 23622320 | tf_op jit(solution)/shard_map/pallas_call | solution.py:195
  1114.4 5.8 pad_maximum_fusion
  1120.2 0.0 all-gather.4.cloned.1.call-done.dir_ref
  1120.2 27.4 %shard_map.152 = bf16[2,2048,5632]{2,1,0:T(8,128)(2,1)} custom-call(bf16[2,2048,5632]{2,1,0:T(8,128)(2,1)} %up_ref.7, bf16[2,2048,512]{2,1,0:T(8,128)(2,1)} %p_ref.7, bf16[5632,512]{1,0:T(8,128)(2,1)} %all-gather.4.cloned.1.call-done.dir_ref, bf16[2,2048,5632]{2,1,0:T(8,128)(2,1)} %shard_map.151.rest_0_), custom_call_target="tpu_custom_call", output_to_operand_aliasing={{}: (3, {})} | custom-call | flops 11811160064 | bytes 23622320 | tf_op jit(solution)/shard_map/pallas_call | solution.py:177
Async XLA Ops:
  7.2 691.9 %reduce-scatter.4.cloned.1.call-start = ((), (), s32[]{:S(2)}) async-start(), calls=%async_computation.3 | async-start | bytes 25952256 | tf_op jit(solution)/shard_map/reduce_scatter | solution.py:216
  558.1 298.2 %reduce-scatter.6.cloned.1.call-start = ((), (), s32[]{:S(2)}) async-start(), calls=%async_computation.4 | async-start | bytes 12976128 | tf_op jit(solution)/shard_map/reduce_scatter | solution.py:216
  668.9 30.1 %copy-start.2 = (f32[2,704,512]{2,1,0:T(8,128)S(1)}, f32[2,704,512]{2,1,0:T(8,128)}, u32[]{:S(2)}) copy-start(f32[2,704,512]{2,1,0:T(8,128)} %param.19) | copy-start | bytes 8650756
  739.4 230.9 %reduce-scatter.8.cloned.1.call-start = ((), (), s32[]{:S(2)}) async-start(), calls=%async_computation.5 | async-start | bytes 12976128 | tf_op jit(solution)/shard_map/reduce_scatter | solution.py:216
  891.2 142.8 %all-gather.6.cloned.1.call-start = ((), (), s32[]{:S(2)}) async-start(), calls=%async_computation.7 | async-start | bytes 12976128 | tf_op jit(solution)/shard_map/all_gather | solution.py:219
  891.8 195.8 %all-gather.8.cloned.1.call-start = ((), (), s32[]{:S(2)}) async-start(), calls=%async_computation.8 | async-start | bytes 6488064 | tf_op jit(solution)/shard_map/all_gather | solution.py:219
  892.4 227.9 %all-gather.4.cloned.1.call-start = ((), (), s32[]{:S(2)}) async-start(), calls=%async_computation.6 | async-start | bytes 6488064 | tf_op jit(solution)/shard_map/all_gather | solution.py:219
  970.3 5.2 copy-start
  970.3 5.2 copy-start.1
Sparse Core Ops, SparseCore 0:
  558.2 140.8 reduce-scatter.3
  739.5 78.7 reduce-scatter.5
  891.3 78.9 reduce-scatter.7
  972.0 61.9 all-gather.5
  1035.7 37.6 all-gather.7
  1075.0 37.6 all-gather.3

commit v2 on v1

--- a/solution.py
+++ b/solution.py
@@ -75,19 +75,29 @@
         4 * rows * d * (ff + rank))(h, dh, w_up, w_down, proj_up, proj_down)
 
 
-def project_pair(act, v, dz, u):
-    rows, ff = act.shape
-    rank = v.shape[1]
-    bn = 512
-
-    def body(act_ref, v_ref, dz_ref, u_ref, out_ref):
-        out_ref[:, :rank] = dot_tn(act_ref[...], v_ref[...])
-        out_ref[:, rank:] = dot_tn(dz_ref[...], u_ref[...])
-
-    col = pl.BlockSpec((rows, bn), lambda j: (0, j))
-    full = pl.BlockSpec((rows, rank), lambda j: (0, 0))
-    return call(body, (ff // bn,), [col, full, col, full], pl.BlockSpec((bn, 2 * rank), lambda j: (j, 0)),
-                jax.ShapeDtypeStruct((ff, 2 * rank), F32), 4 * rows * ff * rank)(act, v, dz, u)
+def back_to_zero(dh, dz, w_up, proj_down):
+    rows, d = dh.shape
+    ff = dz.shape[1]
+    rank = proj_down.shape[2]
+    bm, bn = 1024, 512
+    last = d // bn - 1
+
+    def body(dh_ref, dz_ref, up_ref, q_ref, g_ref, v_ref):
+        n = pl.program_id(1)
+        back = dot_nt(dz_ref[...], up_ref[0])
+        g_ref[:, pl.ds(pl.multiple_of(n * bn, bn), bn)] = (dh_ref[...].astype(F32) + back).astype(BF16)
+
+        @pl.when(n == last)
+        def _():
+            v_ref[...] = dot_nn(g_ref[...], q_ref[0]).astype(BF16)
+
+    return call(
+        body, (rows // bm, d // bn),
+        [pl.BlockSpec((bm, bn), lambda i, n: (i, n)), pl.BlockSpec((bm, ff), lambda i, n: (i, 0)),
+         pl.BlockSpec((1, bn, ff), lambda i, n: (1, n, 0)), pl.BlockSpec((1, d, rank), lambda i, n: (0, 0, 0))],
+        [pl.BlockSpec((bm, d), lambda i, n: (i, 0)), pl.BlockSpec((bm, rank), lambda i, n: (i, 0))],
+        [jax.ShapeDtypeStruct((rows, d), BF16), jax.ShapeDtypeStruct((rows, rank), BF16)],
+        2 * rows * d * (ff + rank))(dh, dz, w_up, proj_down)
 
 
 def layer_zero_forward(x, w_up, proj_up):
@@ -163,10 +173,9 @@
             g1, u, w_down, slope, *extra)
 
 
-def update_up(layer, w_up, proj_up, dirs, at, old, order):
+def update_up(layer, w_up, proj_up, dirs, at, old, order, bn=512):
     d, ff = w_up.shape[1:]
     rank = proj_up.shape[2]
-    bn = 512
     scale = LEARN_RATE * ALPHA_SCALE
 
     def body(up_ref, p_ref, dir_ref, *rest):
@@ -210,8 +219,6 @@
 
 def solution(mesh):
     def local_step(x, dh, w_up, w_down, proj_up, proj_down, mom_up, var_up, mom_down, var_down):
-        rank = proj_up.shape[2]
-
         def scatter(part):
             return lax.psum_scatter(part, 'data', scatter_dimension=0, tiled=True)
 
@@ -221,12 +228,12 @@
         a0, slope0, u0 = layer_zero_forward(x, w_up, proj_up)
         h1 = (x + dot_nn(a0, w_down[0])).astype(BF16)
         a1, dz1, u1, v1 = layer_one(h1, dh, w_up, w_down, proj_up, proj_down)
-        red1 = scatter(project_pair(a1, v1, dz1, u1))
-        g1 = (dh + dot_nt(dz1, w_up[1])).astype(BF16)
-        v0 = dot_nn(g1, proj_down[0]).astype(BF16)
-
-        down1 = adam(mom_down[1], var_down[1], red1[:, :rank])
-        up1 = adam(mom_up[1].T, var_up[1].T, red1[:, rank:])
+        part_down1 = project_one(a1, v1, ())
+        part_up1 = project_one(dz1, u1, (part_down1,))
+        g1, v0 = back_to_zero(dh, dz1, w_up, proj_down)
+
+        down1 = adam(mom_down[1], var_down[1], scatter(part_down1))
+        up1 = adam(mom_up[1].T, var_up[1].T, scatter(part_up1))
         dir1 = jnp.concatenate([down1[2], up1[2]], axis=1)
         dirs1 = gather(dir1)
 
@@ -241,7 +248,7 @@
         new_up = update_up(1, w_up, proj_up, dirs1, 1, (), (part,))
         new_down = update_down(1, w_down, proj_down, dirs1, 0, (), (part,))
         new_down = update_down(0, w_down, proj_down, dirs_down0, 0, (new_down,), ())
-        new_up = update_up(0, w_up, proj_up, dirs_up0, 0, (new_up,), ())
+        new_up = update_up(0, w_up, proj_up, dirs_up0, 0, (new_up,), (), w_up.shape[2] // 4)
         return (new_up, new_down, jnp.stack([up0[0].T, up1[0].T]), jnp.stack([up0[1].T, up1[1].T]),
                 jnp.stack([down0[0], down1[0]]), jnp.stack([down0[1], down1[1]]))
 

time: 1160 us -> 1160 us (level)
  matrix products: 232 us -> 106 us
  Pallas kernels: 731 us -> 855 us
    dot_general x1 -> x0, matrix products: 111 us -> none  [dot_nt(): lax.dot_general(lhs, rhs, (((1,), (1,)), ((), ())), preferred_element_typ...]
    pallas_call x1 -> x3, Pallas kernels: 31.6 us -> 97.1 us  [project_one(): call(body, (ff // bn,), [pl.BlockSpec((rows, bn), lambda j: (0, j)), pl.B...]
    pallas_call x1, Pallas kernels: 57.2 us -> 119 us  [back_to_zero(): call(body, (rows // bm, d // bn), [pl.BlockSpec((bm, bn), lambda i, n: (i...]
    dot_general x2 -> x1, matrix products: 121 us -> 106 us  [dot_nn(): return jnp.dot(lhs, rhs, preferred_element_type=F32)]
    reduce_scatter x3 -> x4, waiting for transfers between devices: 93 us -> 83.2 us  [scatter(): return lax.psum_scatter(part, 'data', scatter_dimension=0, tiled=True)]
  transfers between devices with their start and end apart: 6 -> 7, of which waited for: 3 -> 3; matrix products, arithmetic and copies ran while one was open for 12% -> 2% of each run, Pallas kernels for 17% -> 30%
where the time goes in v2:
time: 1160 us; the launch traced here: 1150 us
  Pallas kernels  855 us (74%)
  waiting for transfers between devices  138 us (12%)
  matrix products  106 us (9%)
  other arithmetic  32.5 us (3%)
  between operations  14.3 us (1%)
    pallas_call x1, Pallas kernels, layer_one(): call(body, (rows // bm, ff // bn), [pl.BlockSpec((bm, d), lambda i, j: (i...  231 us
    pallas_call x1, Pallas kernels, layer_zero_forward(): call(body, (rows // bm, ff // bn), [pl.BlockSpec((bm, d), lambda i, j: (i...  156 us
    pallas_call x2, Pallas kernels, layer_zero_backward(): call(body, (count, rows // bm), [pl.BlockSpec((bm, d), lambda j, i: (i, 0...  147 us
    pallas_call x1, Pallas kernels, back_to_zero(): call(body, (rows // bm, d // bn), [pl.BlockSpec((bm, bn), lambda i, n: (i...  119 us
    dot_general x1, matrix products, dot_nn(): return jnp.dot(lhs, rhs, preferred_element_type=F32)  106 us
    pallas_call x3, Pallas kernels, project_one(): call(body, (ff // bn,), [pl.BlockSpec((rows, bn), lambda j: (0, j)), pl.B...  97.1 us
    reduce_scatter x4, waiting for transfers between devices, scatter(): return lax.psum_scatter(part, 'data', scatter_dimension=0, tiled=True)  83.2 us
    all_gather x3, waiting for transfers between devices, gather(): return lax.all_gather(part, 'data', axis=0, tiled=True)  53.5 us
  transfers between devices with their start and end apart: 7, of which 3 were waited for; matrix products, arithmetic and copies ran while one was open for 2% of the time, Pallas kernels for 30%

profile of v2, /device:TPU:0, one launch (start us, length us, event | category | flops | bytes accessed | tf_op | source)
XLA Modules:
  0.0 1146.7 jit_solution(9767818592324226945)
XLA Ops:
  7.2 0.0 reduce-scatter.5.cloned.1.call-start
  7.2 156.3 %shard_map.145 = (bf16[4096,5632]{1,0:T(8,128)(2,1)}, f32[4096,5632]{1,0:T(8,128)}, bf16[4096,512]{1,0:T(8,128)(2,1)}) custom-call(bf16[4096,2048]{1,0:T(8,128)(2,1)} %x_ref.1, bf16[2,2048,5632]{2,1,0:T(8,128)(2,1)} %up_ref.9, bf16[2,2048,512]{2,1,0:T(8,128)(2,1)} %p_ref.7), custom_call_target="tpu_custom_call" | custom-call | flops 103079215104 | bytes 206158432 | tf_op jit(solution)/shard_map/pallas_call | solution.py:118
  163.5 106.3 %add_convert_fusion.h_ref = bf16[4096,2048]{1,0:T(8,128)(2,1)} fusion(bf16[4096,2048]{1,0:T(8,128)(2,1)} %x_ref.1, bf16[4096,5632]{1,0:T(8,128)(2,1)} %get-tuple-element.15.act_ref, bf16[2,5632,2048]{2,1,0:T(8,128)(2,1)} %down_ref.9), kind=kOutput, calls=%fused_computation | convolution fusion | flops 94514446336 | bytes 102760448 | tf_op jit(solution)/shard_map/dot_general | solution.py:23
  269.8 231.0 %shard_map.146 = (bf16[4096,5632]{1,0:T(8,128)(2,1)}, bf16[4096,5632]{1,0:T(8,128)(2,1)}, bf16[4096,512]{1,0:T(8,128)(2,1)}, bf16[4096,512]{1,0:T(8,128)(2,1)}) custom-call(bf16[4096,2048]{1,0:T(8,128)(2,1)} %add_convert_fusion.h_ref, bf16[4096,2048]{1,0:T(8,128)(2,1)} %dh_ref.3, bf16[2,2048,5632]{2,1,0:T(8,128)(2,1)} %up_ref.9, ...), custom_call_target="tpu_custom_call" | custom-call | flops 206158430208 | bytes 412316864 | tf_op jit(solution)/shard_map/pallas_call | solution.py:68
  500.8 31.6 %shard_map.149.rest_0_ = f32[5632,512]{1,0:T(8,128)} custom-call(bf16[4096,5632]{1,0:T(8,128)(2,1)} %get-tuple-element.21.act_ref, bf16[4096,512]{1,0:T(8,128)(2,1)} %get-tuple-element.22.v_ref), custom_call_target="tpu_custom_call" | custom-call | flops 23622320128 | bytes 47244640 | tf_op jit(solution)/shard_map/pallas_call | solution.py:136
  532.4 0.0 reduce-scatter.5.cloned.1.call-update
  532.4 0.0 reduce-scatter.7.cloned.1.call-start
  532.5 34.0 %shard_map.150 = f32[5632,512]{1,0:T(8,128)} custom-call(bf16[4096,5632]{1,0:T(8,128)(2,1)} %get-tuple-element.16.dz_ref.act_ref, bf16[4096,512]{1,0:T(8,128)(2,1)} %get-tuple-element.23.v_ref, f32[5632,512]{1,0:T(8,128)} %shard_map.149.rest_0_), custom_call_target="tpu_custom_call" | custom-call | flops 23622320128 | bytes 47244640 | tf_op jit(solution)/shard_map/pallas_call | solution.py:136
  566.5 0.0 reduce-scatter.7.cloned.1.call-update
  566.5 0.0 reduce-scatter.9.cloned.1.call-start
  566.5 119.2 %shard_map.147 = (bf16[4096,2048]{1,0:T(8,128)(2,1)}, bf16[4096,512]{1,0:T(8,128)(2,1)}) custom-call(bf16[4096,2048]{1,0:T(8,128)(2,1)} %dh_ref.3, bf16[4096,5632]{1,0:T(8,128)(2,1)} %get-tuple-element.16.dz_ref.act_ref, bf16[2,2048,5632]{2,1,0:T(8,128)(2,1)} %up_ref.9, bf16[2,2048,512]{2,1,0:T(8,128)(2,1)} %q_ref.7), custom_call_target="tpu_custom_call" | custom-call | flops 103079215104 | bytes 206158432 | tf_op jit(solution)/shard_map/pallas_call | solution.py:94
  685.7 0.0 copy-start.2
  685.7 0.0 reduce-scatter.5.cloned.1.call-done
  685.7 5.2 fusion.16
  690.9 5.5 reduce-scatter.7.cloned.1.call-done
  696.5 0.0 copy-done.2
  696.5 0.0 copy-start.3
  696.5 4.4 fusion.15
  700.9 0.0 copy-done.3
  700.9 1.3 pad_maximum_fusion.4.rest_0_
  702.2 31.5 %shard_map.151 = f32[5632,512]{1,0:T(8,128)} custom-call(bf16[4096,5632]{1,0:T(8,128)(2,1)} %get-tuple-element.15.act_ref, bf16[4096,512]{1,0:T(8,128)(2,1)} %get-tuple-element.20.v_ref, bf16[704,1024]{1,0:T(8,128)(2,1)} %pad_maximum_fusion.4.rest_0_), custom_call_target="tpu_custom_call" | custom-call | flops 23622320128 | bytes 47244640 | tf_op jit(solution)/shard_map/pallas_call | solution.py:136
  733.7 0.0 reduce-scatter.9.cloned.1.call-update
  733.7 0.0 reduce-scatter.11.cloned.1.call-start
  733.8 116.8 %shard_map.148.rest_0_ = f32[5632,512]{1,0:T(8,128)} custom-call(bf16[4096,2048]{1,0:T(8,128)(2,1)} %get-tuple-element.17.g_ref, bf16[4096,512]{1,0:T(8,128)(2,1)} %get-tuple-element.18.u_ref, bf16[2,5632,2048]{2,1,0:T(8,128)(2,1)} %down_ref.9, f32[4096,5632]{1,0:T(8,128)} %get-tuple-element.19.slope_ref), custom_call_target="tpu_custom_call" | custom-call | flops 96636764160 | bytes 193273536 | tf_op jit(solution)/shard_map/pallas_call | solution.py:164
  850.5 0.0 reduce-scatter.9.cloned.1.call-done
  850.5 5.0 fusion.14
  855.6 29.8 %shard_map.152.rest_0_ = f32[5632,512]{1,0:T(8,128)} custom-call(bf16[4096,2048]{1,0:T(8,128)(2,1)} %get-tuple-element.17.g_ref, bf16[4096,512]{1,0:T(8,128)(2,1)} %get-tuple-element.18.u_ref, bf16[2,5632,2048]{2,1,0:T(8,128)(2,1)} %down_ref.9, f32[4096,5632]{1,0:T(8,128)} %get-tuple-element.19.slope_ref, ...), custom_call_target="tpu_custom_call", output_to_operand_aliasing={{}: (4, {})} | custom-call | flops 21474836480 | bytes 42949672 | tf_op jit(solution)/shard_map/pallas_call | solution.py:164
  885.4 0.0 reduce-scatter.11.cloned.1.call-update
  885.4 0.0 all-gather.6.cloned.1.call-start
  885.5 0.5 all-gather.6.cloned.1.call-update
  886.0 0.0 all-gather.8.cloned.1.call-start
  886.1 0.5 all-gather.8.cloned.1.call-update
  886.6 0.2 all-gather.4.cloned.1.call-start
  886.8 77.7 %reduce-scatter.11.cloned.1.call-done = f32[704,512]{1,0:T(8,128)} async-done(((f32[5632,512]{1,0:T(8,128)}), f32[704,512]{1,0:T(8,128)}) %reduce-scatter.11.cloned.1.call-update) | async-done | bytes 1441808 | tf_op jit(solution)/shard_map/reduce_scatter | solution.py:223
  964.5 0.0 copy-start
  964.5 0.0 copy-start.1
  964.5 5.2 fusion.13
  969.7 0.0 all-gather.4.cloned.1.call-update
  969.7 0.0 copy-done
  969.7 0.0 copy-done.1
  969.7 5.6 pad_maximum_fusion.2
  975.4 53.4 %all-gather.6.cloned.1.call-done.dir_ref = bf16[5632,1024]{1,0:T(8,128)(2,1)} async-done(((bf16[704,1024]{1,0:T(8,128)(2,1)}), bf16[5632,1024]{1,0:T(8,128)(2,1)}) %all-gather.6.cloned.1.call-update) | async-done | bytes 11534352 | tf_op jit(solution)/shard_map/all_gather | solution.py:226
  1028.8 26.3 %shard_map.155.rest_0_ = bf16[2,5632,2048]{2,1,0:T(8,128)(2,1)} custom-call(bf16[2,5632,2048]{2,1,0:T(8,128)(2,1)} %down_ref.9, bf16[2,2048,512]{2,1,0:T(8,128)(2,1)} %q_ref.7, bf16[5632,1024]{1,0:T(8,128)(2,1)} %all-gather.6.cloned.1.call-done.dir_ref, f32[5632,512]{1,0:T(8,128)} %shard_map.152.rest_0_), custom_call_target="tpu_custom_call" | custom-call | flops 11811160064 | bytes 23622320 | tf_op jit(solution)/shard_map/pallas_call | solution.py:204
  1055.1 27.2 %shard_map.153.rest_0_ = bf16[2,2048,5632]{2,1,0:T(8,128)(2,1)} custom-call(bf16[2,2048,5632]{2,1,0:T(8,128)(2,1)} %up_ref.9, bf16[2,2048,512]{2,1,0:T(8,128)(2,1)} %p_ref.7, bf16[5632,1024]{1,0:T(8,128)(2,1)} %all-gather.6.cloned.1.call-done.dir_ref, f32[5632,512]{1,0:T(8,128)} %shard_map.152.rest_0_), custom_call_target="tpu_custom_call" | custom-call | flops 11811160064 | bytes 23622320 | tf_op jit(solution)/shard_map/pallas_call | solution.py:186
  1082.3 0.0 all-gather.8.cloned.1.call-done.dir_ref
  1082.3 26.2 %shard_map.156 = bf16[2,5632,2048]{2,1,0:T(8,128)(2,1)} custom-call(bf16[2,5632,2048]{2,1,0:T(8,128)(2,1)} %down_ref.9, bf16[2,2048,512]{2,1,0:T(8,128)(2,1)} %q_ref.7, bf16[5632,512]{1,0:T(8,128)(2,1)} %all-gather.8.cloned.1.call-done.dir_ref, bf16[2,5632,2048]{2,1,0:T(8,128)(2,1)} %shard_map.155.rest_0_), custom_call_target="tpu_custom_call", output_to_operand_aliasing={{}: (3, {})} | custom-call | flops 11811160064 | bytes 23622320 | tf_op jit(solution)/shard_map/pallas_call | solution.py:204
  1108.5 5.8 pad_maximum_fusion
  1114.3 0.0 all-gather.4.cloned.1.call-done.dir_ref
  1114.3 25.3 %shard_map.154 = bf16[2,2048,5632]{2,1,0:T(8,128)(2,1)} custom-call(bf16[2,2048,5632]{2,1,0:T(8,128)(2,1)} %up_ref.9, bf16[2,2048,512]{2,1,0:T(8,128)(2,1)} %p_ref.7, bf16[5632,512]{1,0:T(8,128)(2,1)} %all-gather.4.cloned.1.call-done.dir_ref, bf16[2,2048,5632]{2,1,0:T(8,128)(2,1)} %shard_map.153.rest_0_), custom_call_target="tpu_custom_call", output_to_operand_aliasing={{}: (3, {})} | custom-call | flops 11811160064 | bytes 23622320 | tf_op jit(solution)/shard_map/pallas_call | solution.py:186
Async XLA Ops:
  7.2 678.6 %reduce-scatter.5.cloned.1.call-start = ((), (), s32[]{:S(2)}) async-start(), calls=%async_computation.4 | async-start | bytes 12976128 | tf_op jit(solution)/shard_map/reduce_scatter | solution.py:223
  532.4 164.0 %reduce-scatter.7.cloned.1.call-start = ((), (), s32[]{:S(2)}) async-start(), calls=%async_computation.5 | async-start | bytes 12976128 | tf_op jit(solution)/shard_map/reduce_scatter | solution.py:223
  566.5 284.1 %reduce-scatter.9.cloned.1.call-start = ((), (), s32[]{:S(2)}) async-start(), calls=%async_computation.6 | async-start | bytes 12976128 | tf_op jit(solution)/shard_map/reduce_scatter | solution.py:223
  685.7 10.7 copy-start.2
  696.5 4.4 copy-start.3
  733.7 230.8 %reduce-scatter.11.cloned.1.call-start = ((), (), s32[]{:S(2)}) async-start(), calls=%async_computation.7 | async-start | bytes 12976128 | tf_op jit(solution)/shard_map/reduce_scatter | solution.py:223
  885.4 143.4 %all-gather.6.cloned.1.call-start = ((), (), s32[]{:S(2)}) async-start(), calls=%async_computation.9 | async-start | bytes 12976128 | tf_op jit(solution)/shard_map/all_gather | solution.py:226
  886.0 196.3 %all-gather.8.cloned.1.call-start = ((), (), s32[]{:S(2)}) async-start(), calls=%async_computation.10 | async-start | bytes 6488064 | tf_op jit(solution)/shard_map/all_gather | solution.py:226
  886.6 227.7 %all-gather.4.cloned.1.call-start = ((), (), s32[]{:S(2)}) async-start(), calls=%async_computation.8 | async-start | bytes 6488064 | tf_op jit(solution)/shard_map/all_gather | solution.py:226
  964.5 5.2 copy-start
  964.5 5.2 copy-start.1
Sparse Core Ops, SparseCore 0:
  532.6 81.5 reduce-scatter.4
  617.6 78.8 reduce-scatter.6
  733.8 78.7 reduce-scatter.8
  885.6 78.9 reduce-scatter.10
  966.8 61.9 all-gather.5
  1030.5 37.6 all-gather.7
  1069.9 37.6 all-gather.3

commit v3 on v2

--- a/solution.py
+++ b/solution.py
@@ -100,29 +100,37 @@
         2 * rows * d * (ff + rank))(dh, dz, w_up, proj_down)
 
 
-def layer_zero_forward(x, w_up, proj_up):
+def layer_zero_forward(x, w_up):
     rows, d = x.shape
     ff = w_up.shape[2]
-    rank = proj_up.shape[2]
-    bm, bn = 2048, 512
-
-    def body(x_ref, up_ref, p_ref, act_ref, slope_ref, u_ref):
+    bm, bn = 1024, 512
+
+    def body(x_ref, up_ref, act_ref, slope_ref):
         g, dg = gelu_parts(dot_nn(x_ref[...], up_ref[0]))
         act_ref[...] = g.astype(BF16)
         slope_ref[...] = dg
 
-        @pl.when(pl.program_id(1) == 0)
-        def _():
-            u_ref[...] = dot_nn(x_ref[...], p_ref[0]).astype(BF16)
-
     return call(
         body, (rows // bm, ff // bn),
-        [pl.BlockSpec((bm, d), lambda i, j: (i, 0)), pl.BlockSpec((1, d, bn), lambda i, j: (0, 0, j)),
-         pl.BlockSpec((1, d, rank), lambda i, j: (0, 0, 0))],
-        [pl.BlockSpec((bm, bn), lambda i, j: (i, j))] * 2 + [pl.BlockSpec((bm, rank), lambda i, j: (i, 0))],
-        [jax.ShapeDtypeStruct((rows, ff), BF16), jax.ShapeDtypeStruct((rows, ff), F32),
-         jax.ShapeDtypeStruct((rows, rank), BF16)],
-        2 * rows * d * (ff + rank))(x, w_up, proj_up)
+        [pl.BlockSpec((bm, d), lambda i, j: (i, 0)), pl.BlockSpec((1, d, bn), lambda i, j: (0, 0, j))],
+        [pl.BlockSpec((bm, bn), lambda i, j: (i, j))] * 2,
+        [jax.ShapeDtypeStruct((rows, ff), BF16), jax.ShapeDtypeStruct((rows, ff), F32)],
+        2 * rows * d * ff)(x, w_up)
+
+
+def project_rows(layer, h, proj, order):
+    rows, d = h.shape
+    rank = proj.shape[2]
+    bm = 1024
+
+    def body(h_ref, p_ref, *rest):
+        rest[-1][...] = dot_nn(h_ref[...], p_ref[0]).astype(BF16)
+
+    return call(body, (rows // bm,),
+                [pl.BlockSpec((bm, d), lambda i: (i, 0)), pl.BlockSpec((1, d, rank), lambda i: (layer, 0, 0))]
+                + [pl.BlockSpec(memory_space=pl.ANY)] * len(order),
+                pl.BlockSpec((bm, rank), lambda i: (i, 0)),
+                jax.ShapeDtypeStruct((rows, rank), BF16), 2 * rows * d * rank)(h, proj, *order)
 
 
 def project_one(act, v, order):
@@ -225,11 +233,12 @@
         def gather(part):
             return lax.all_gather(part, 'data', axis=0, tiled=True)
 
-        a0, slope0, u0 = layer_zero_forward(x, w_up, proj_up)
+        a0, slope0 = layer_zero_forward(x, w_up)
         h1 = (x + dot_nn(a0, w_down[0])).astype(BF16)
         a1, dz1, u1, v1 = layer_one(h1, dh, w_up, w_down, proj_up, proj_down)
         part_down1 = project_one(a1, v1, ())
         part_up1 = project_one(dz1, u1, (part_down1,))
+        u0 = project_rows(0, x, proj_up, (part_up1,))
         g1, v0 = back_to_zero(dh, dz1, w_up, proj_down)
 
         down1 = adam(mom_down[1], var_down[1], scatter(part_down1))
@@ -240,8 +249,8 @@
         down0 = adam(mom_down[0], var_down[0], scatter(project_one(a0, v0, (dir1,))))
         dirs_down0 = gather(down0[2])
         blocks = w_up.shape[2] // 512
-        part = layer_zero_backward(g1, u0, w_down, slope0, 0, blocks - 2, (), ())
-        part = layer_zero_backward(g1, u0, w_down, slope0, blocks - 2, 2, (part,), (down0[2],))
+        part = layer_zero_backward(g1, u0, w_down, slope0, 0, blocks - 3, (), ())
+        part = layer_zero_backward(g1, u0, w_down, slope0, blocks - 3, 3, (part,), (down0[2],))
         up0 = adam(mom_up[0].T, var_up[0].T, scatter(part))
         dirs_up0 = gather(up0[2])
 

time: 1160 us -> 1160 us (level)
    pallas_call x0 -> x1, Pallas kernels: none -> 15.6 us  [project_rows(): call(body, (rows // bm,), [pl.BlockSpec((bm, d), lambda i: (i, 0)), pl.Bl...]
    pallas_call x1, Pallas kernels: 156 us -> 144 us  [layer_zero_forward(): call(body, (rows // bm, ff // bn), [pl.BlockSpec((bm, d), lambda i, j: (i...]
  transfers between devices with their start and end apart: 7 -> 7, of which waited for: 3 -> 3; matrix products, arithmetic and copies ran while one was open for 2% -> 2% of each run, Pallas kernels for 30% -> 31%
where the time goes in v3:
time: 1160 us; the launch traced here: 1150 us
  Pallas kernels  855 us (74%)
  waiting for transfers between devices  138 us (12%)
  matrix products  106 us (9%)
  other arithmetic  32.5 us (3%)
  between operations  14.7 us (1%)
    pallas_call x1, Pallas kernels, layer_one(): call(body, (rows // bm, ff // bn), [pl.BlockSpec((bm, d), lambda i, j: (i...  231 us
    pallas_call x1, Pallas kernels, layer_zero_forward(): call(body, (rows // bm, ff // bn), [pl.BlockSpec((bm, d), lambda i, j: (i...  144 us
    pallas_call x2, Pallas kernels, layer_zero_backward(): call(body, (count, rows // bm), [pl.BlockSpec((bm, d), lambda j, i: (i, 0...  143 us
    pallas_call x1, Pallas kernels, back_to_zero(): call(body, (rows // bm, d // bn), [pl.BlockSpec((bm, bn), lambda i, n: (i...  119 us
    dot_general x1, matrix products, dot_nn(): return jnp.dot(lhs, rhs, preferred_element_type=F32)  106 us
    pallas_call x3, Pallas kernels, project_one(): call(body, (ff // bn,), [pl.BlockSpec((rows, bn), lambda j: (0, j)), pl.B...  96.9 us
    reduce_scatter x4, waiting for transfers between devices, scatter(): return lax.psum_scatter(part, 'data', scatter_dimension=0, tiled=True)  83.5 us
    pallas_call x2, Pallas kernels, update_down(): call(body, (ff // bn,), [block, pl.BlockSpec((1, d, rank), lambda j: (lay...  53.7 us
  transfers between devices with their start and end apart: 7, of which 3 were waited for; matrix products, arithmetic and copies ran while one was open for 2% of the time, Pallas kernels for 31%

profile of v3, /device:TPU:0, one launch (start us, length us, event | category | flops | bytes accessed | tf_op | source)
XLA Modules:
  0.0 1146.9 jit_solution(5254488976844915211)
XLA Ops:
  7.2 0.0 reduce-scatter.5.cloned.1.call-start
  7.2 143.5 %shard_map.145 = (bf16[4096,5632]{1,0:T(8,128)(2,1)}, f32[4096,5632]{1,0:T(8,128)}) custom-call(bf16[4096,2048]{1,0:T(8,128)(2,1)} %h_ref.1, bf16[2,2048,5632]{2,1,0:T(8,128)(2,1)} %up_ref.9), custom_call_target="tpu_custom_call" | custom-call | flops 94489280512 | bytes 188978560 | tf_op jit(solution)/shard_map/pallas_call | solution.py:113
  150.7 106.1 %add_convert_fusion.h_ref = bf16[4096,2048]{1,0:T(8,128)(2,1)} fusion(bf16[4096,2048]{1,0:T(8,128)(2,1)} %h_ref.1, bf16[4096,5632]{1,0:T(8,128)(2,1)} %get-tuple-element.14.act_ref, bf16[2,5632,2048]{2,1,0:T(8,128)(2,1)} %down_ref.9), kind=kOutput, calls=%fused_computation | convolution fusion | flops 94514446336 | bytes 102760448 | tf_op jit(solution)/shard_map/dot_general | solution.py:23
  256.8 231.1 %shard_map.146 = (bf16[4096,5632]{1,0:T(8,128)(2,1)}, bf16[4096,5632]{1,0:T(8,128)(2,1)}, bf16[4096,512]{1,0:T(8,128)(2,1)}, bf16[4096,512]{1,0:T(8,128)(2,1)}) custom-call(bf16[4096,2048]{1,0:T(8,128)(2,1)} %add_convert_fusion.h_ref, bf16[4096,2048]{1,0:T(8,128)(2,1)} %dh_ref.3, bf16[2,2048,5632]{2,1,0:T(8,128)(2,1)} %up_ref.9, ...), custom_call_target="tpu_custom_call" | custom-call | flops 206158430208 | bytes 412316864 | tf_op jit(solution)/shard_map/pallas_call | solution.py:68
  487.9 31.7 %shard_map.148.rest_0_ = f32[5632,512]{1,0:T(8,128)} custom-call(bf16[4096,5632]{1,0:T(8,128)(2,1)} %get-tuple-element.18.act_ref, bf16[4096,512]{1,0:T(8,128)(2,1)} %get-tuple-element.19.v_ref), custom_call_target="tpu_custom_call" | custom-call | flops 23622320128 | bytes 47244640 | tf_op jit(solution)/shard_map/pallas_call | solution.py:144
  519.6 0.0 reduce-scatter.5.cloned.1.call-update
  519.7 0.0 reduce-scatter.7.cloned.1.call-start
  519.7 33.7 %shard_map.149.rest_0_ = f32[5632,512]{1,0:T(8,128)} custom-call(bf16[4096,5632]{1,0:T(8,128)(2,1)} %get-tuple-element.15.dz_ref.act_ref, bf16[4096,512]{1,0:T(8,128)(2,1)} %get-tuple-element.17.v_ref, f32[5632,512]{1,0:T(8,128)} %shard_map.148.rest_0_), custom_call_target="tpu_custom_call" | custom-call | flops 23622320128 | bytes 47244640 | tf_op jit(solution)/shard_map/pallas_call | solution.py:144
  553.4 0.0 reduce-scatter.7.cloned.1.call-update
  553.4 0.0 reduce-scatter.9.cloned.1.call-start
  553.4 119.2 %shard_map.147 = (bf16[4096,2048]{1,0:T(8,128)(2,1)}, bf16[4096,512]{1,0:T(8,128)(2,1)}) custom-call(bf16[4096,2048]{1,0:T(8,128)(2,1)} %dh_ref.3, bf16[4096,5632]{1,0:T(8,128)(2,1)} %get-tuple-element.15.dz_ref.act_ref, bf16[2,2048,5632]{2,1,0:T(8,128)(2,1)} %up_ref.9, bf16[2,2048,512]{2,1,0:T(8,128)(2,1)} %q_ref.7), custom_call_target="tpu_custom_call" | custom-call | flops 103079215104 | bytes 206158432 | tf_op jit(solution)/shard_map/pallas_call | solution.py:94
  672.7 0.0 copy-start.2
  672.7 0.0 reduce-scatter.5.cloned.1.call-done
  672.7 5.2 fusion.16
  677.8 5.8 reduce-scatter.7.cloned.1.call-done
  683.7 0.0 copy-done.2
  683.7 0.0 copy-start.3
  683.7 4.4 fusion.15
  688.1 0.0 copy-done.3
  688.1 1.3 pad_maximum_fusion.4.rest_0_
  689.4 31.5 %shard_map.152 = f32[5632,512]{1,0:T(8,128)} custom-call(bf16[4096,5632]{1,0:T(8,128)(2,1)} %get-tuple-element.14.act_ref, bf16[4096,512]{1,0:T(8,128)(2,1)} %get-tuple-element.21.v_ref, bf16[704,1024]{1,0:T(8,128)(2,1)} %pad_maximum_fusion.4.rest_0_), custom_call_target="tpu_custom_call" | custom-call | flops 23622320128 | bytes 47244640 | tf_op jit(solution)/shard_map/pallas_call | solution.py:144
  720.9 0.0 reduce-scatter.9.cloned.1.call-update
  720.9 0.0 reduce-scatter.11.cloned.1.call-start
  721.0 15.6 %shard_map.150.u_ref = bf16[4096,512]{1,0:T(8,128)(2,1)} custom-call(bf16[4096,2048]{1,0:T(8,128)(2,1)} %h_ref.1, bf16[2,2048,512]{2,1,0:T(8,128)(2,1)} %p_ref.7, f32[5632,512]{1,0:T(8,128)} %shard_map.149.rest_0_), custom_call_target="tpu_custom_call" | custom-call | flops 8589934592 | bytes 17179868 | tf_op jit(solution)/shard_map/pallas_call | solution.py:129
  736.6 101.0 %shard_map.151.rest_0_ = f32[5632,512]{1,0:T(8,128)} custom-call(bf16[4096,2048]{1,0:T(8,128)(2,1)} %get-tuple-element.16.g_ref, bf16[4096,512]{1,0:T(8,128)(2,1)} %shard_map.150.u_ref, bf16[2,5632,2048]{2,1,0:T(8,128)(2,1)} %down_ref.9, f32[4096,5632]{1,0:T(8,128)} %get-tuple-element.20.slope_ref), custom_call_target="tpu_custom_call" | custom-call | flops 85899345920 | bytes 171798688 | tf_op jit(solution)/shard_map/pallas_call | solution.py:172
  837.6 0.0 reduce-scatter.9.cloned.1.call-done
  837.6 5.1 fusion.14
  842.7 41.7 %shard_map.153.rest_0_ = f32[5632,512]{1,0:T(8,128)} custom-call(bf16[4096,2048]{1,0:T(8,128)(2,1)} %get-tuple-element.16.g_ref, bf16[4096,512]{1,0:T(8,128)(2,1)} %shard_map.150.u_ref, bf16[2,5632,2048]{2,1,0:T(8,128)(2,1)} %down_ref.9, f32[4096,5632]{1,0:T(8,128)} %get-tuple-element.20.slope_ref, ...), custom_call_target="tpu_custom_call", output_to_operand_aliasing={{}: (4, {})} | custom-call | flops 32212254720 | bytes 64424508 | tf_op jit(solution)/shard_map/pallas_call | solution.py:172
  884.4 0.0 reduce-scatter.11.cloned.1.call-update
  884.4 0.0 all-gather.6.cloned.1.call-start
  884.4 0.5 all-gather.6.cloned.1.call-update
  885.0 0.0 all-gather.8.cloned.1.call-start
  885.0 0.5 all-gather.8.cloned.1.call-update
  885.5 0.0 all-gather.4.cloned.1.call-start
  885.6 77.6 %reduce-scatter.11.cloned.1.call-done = f32[704,512]{1,0:T(8,128)} async-done(((f32[5632,512]{1,0:T(8,128)}), f32[704,512]{1,0:T(8,128)}) %reduce-scatter.11.cloned.1.call-update) | async-done | bytes 1441808 | tf_op jit(solution)/shard_map/reduce_scatter | solution.py:231
  963.2 0.0 copy-start
  963.2 0.0 copy-start.1
  963.2 5.1 fusion.13
  968.4 0.0 all-gather.4.cloned.1.call-update
  968.4 0.0 copy-done
  968.4 0.0 copy-done.1
  968.4 5.6 pad_maximum_fusion.2
  974.0 53.5 %all-gather.6.cloned.1.call-done.dir_ref = bf16[5632,1024]{1,0:T(8,128)(2,1)} async-done(((bf16[704,1024]{1,0:T(8,128)(2,1)}), bf16[5632,1024]{1,0:T(8,128)(2,1)}) %all-gather.6.cloned.1.call-update) | async-done | bytes 11534352 | tf_op jit(solution)/shard_map/all_gather | solution.py:234
  1027.5 26.6 %shard_map.156.rest_0_ = bf16[2,5632,2048]{2,1,0:T(8,128)(2,1)} custom-call(bf16[2,5632,2048]{2,1,0:T(8,128)(2,1)} %down_ref.9, bf16[2,2048,512]{2,1,0:T(8,128)(2,1)} %q_ref.7, bf16[5632,1024]{1,0:T(8,128)(2,1)} %all-gather.6.cloned.1.call-done.dir_ref, f32[5632,512]{1,0:T(8,128)} %shard_map.153.rest_0_), custom_call_target="tpu_custom_call" | custom-call | flops 11811160064 | bytes 23622320 | tf_op jit(solution)/shard_map/pallas_call | solution.py:212
  1054.2 27.2 %shard_map.154.rest_0_ = bf16[2,2048,5632]{2,1,0:T(8,128)(2,1)} custom-call(bf16[2,2048,5632]{2,1,0:T(8,128)(2,1)} %up_ref.9, bf16[2,2048,512]{2,1,0:T(8,128)(2,1)} %p_ref.7, bf16[5632,1024]{1,0:T(8,128)(2,1)} %all-gather.6.cloned.1.call-done.dir_ref, f32[5632,512]{1,0:T(8,128)} %shard_map.153.rest_0_), custom_call_target="tpu_custom_call" | custom-call | flops 11811160064 | bytes 23622320 | tf_op jit(solution)/shard_map/pallas_call | solution.py:194
  1081.4 0.0 all-gather.8.cloned.1.call-done.dir_ref
  1081.4 27.1 %shard_map.157 = bf16[2,5632,2048]{2,1,0:T(8,128)(2,1)} custom-call(bf16[2,5632,2048]{2,1,0:T(8,128)(2,1)} %down_ref.9, bf16[2,2048,512]{2,1,0:T(8,128)(2,1)} %q_ref.7, bf16[5632,512]{1,0:T(8,128)(2,1)} %all-gather.8.cloned.1.call-done.dir_ref, bf16[2,5632,2048]{2,1,0:T(8,128)(2,1)} %shard_map.156.rest_0_), custom_call_target="tpu_custom_call", output_to_operand_aliasing={{}: (3, {})} | custom-call | flops 11811160064 | bytes 23622320 | tf_op jit(solution)/shard_map/pallas_call | solution.py:212
  1108.5 5.8 pad_maximum_fusion
  1114.3 0.0 all-gather.4.cloned.1.call-done.dir_ref
  1114.3 25.3 %shard_map.155 = bf16[2,2048,5632]{2,1,0:T(8,128)(2,1)} custom-call(bf16[2,2048,5632]{2,1,0:T(8,128)(2,1)} %up_ref.9, bf16[2,2048,512]{2,1,0:T(8,128)(2,1)} %p_ref.7, bf16[5632,512]{1,0:T(8,128)(2,1)} %all-gather.4.cloned.1.call-done.dir_ref, bf16[2,2048,5632]{2,1,0:T(8,128)(2,1)} %shard_map.154.rest_0_), custom_call_target="tpu_custom_call", output_to_operand_aliasing={{}: (3, {})} | custom-call | flops 11811160064 | bytes 23622320 | tf_op jit(solution)/shard_map/pallas_call | solution.py:194
Async XLA Ops:
  7.2 665.5 %reduce-scatter.5.cloned.1.call-start = ((), (), s32[]{:S(2)}) async-start(), calls=%async_computation.4 | async-start | bytes 12976128 | tf_op jit(solution)/shard_map/reduce_scatter | solution.py:231
  519.7 164.0 %reduce-scatter.7.cloned.1.call-start = ((), (), s32[]{:S(2)}) async-start(), calls=%async_computation.5 | async-start | bytes 12976128 | tf_op jit(solution)/shard_map/reduce_scatter | solution.py:231
  553.4 284.2 %reduce-scatter.9.cloned.1.call-start = ((), (), s32[]{:S(2)}) async-start(), calls=%async_computation.6 | async-start | bytes 12976128 | tf_op jit(solution)/shard_map/reduce_scatter | solution.py:231
  672.7 11.0 copy-start.2
  683.7 4.4 copy-start.3
  720.9 242.3 %reduce-scatter.11.cloned.1.call-start = ((), (), s32[]{:S(2)}) async-start(), calls=%async_computation.7 | async-start | bytes 12976128 | tf_op jit(solution)/shard_map/reduce_scatter | solution.py:231
  884.4 143.1 %all-gather.6.cloned.1.call-start = ((), (), s32[]{:S(2)}) async-start(), calls=%async_computation.9 | async-start | bytes 12976128 | tf_op jit(solution)/shard_map/all_gather | solution.py:234
  885.0 196.4 %all-gather.8.cloned.1.call-start = ((), (), s32[]{:S(2)}) async-start(), calls=%async_computation.10 | async-start | bytes 6488064 | tf_op jit(solution)/shard_map/all_gather | solution.py:234
  885.5 228.8 %all-gather.4.cloned.1.call-start = ((), (), s32[]{:S(2)}) async-start(), calls=%async_computation.8 | async-start | bytes 6488064 | tf_op jit(solution)/shard_map/all_gather | solution.py:234
  963.2 5.2 copy-start
  963.2 5.2 copy-start.1
Sparse Core Ops, SparseCore 0:
  519.8 81.5 reduce-scatter.4
  604.8 78.7 reduce-scatter.6
  721.1 78.7 reduce-scatter.8
  884.5 78.6 reduce-scatter.10
  965.5 61.9 all-gather.5
  1029.2 37.6 all-gather.7
  1068.6 37.6 all-gather.3
